TPU v7x, 32 devices: a whole 2x2x4 slice. The times are simulated.
32 devices in a mesh: pole: 4 (over y, core), dom: 8 (over z, x).
Axes of the slice: x: 2, y: 2, z: 4, core: 2. Of those that a mesh axis runs over, the one named last changes fastest.
Arguments:
- initial_block: bfloat16 [8, 8, 512, 256], P('dom'), may hold values from -24 to 24
- coupling: bfloat16 [8, 8, 512, 512], P('dom'), may hold values from -0.125 to 0.125
- pivots: bfloat16 [4, 8, 8, 2, 512, 512], P('pole', 'dom'), may hold values from -0.125 to 0.125
- interface: bfloat16 [4, 8, 3, 2, 512, 512], P('pole', 'dom'), may hold values from -0.1875 to 0.1875
- pole_values: float32 [4, 4], P('pole'), may hold values from 0.5 to 1.5
Outputs:
- filtered_basis: float32 [8, 8, 512, 256], P('dom', 'pole')
- rayleigh: float32 [256, 256], replicated
All inputs are finite; a program needn't handle non-finite values.
Results may differ from a plain program's by a relative error of at most 0.008.
Values sent between devices are 32-bit elements; how exact they have to be, the bound alone decides.
No kernel may reach another device: no remote copies, remote signals or barrier semaphores. Data moves between devices by JAX's collectives and lax.ppermute only.
A program may use at most 192 MiB of HBM per device.

v0:
```python
import jax
import jax.numpy as jnp
from jax import lax
from jax.sharding import PartitionSpec as P

B = 512
M = 256


def shifted(x, axis, by):
    length = lax.axis_size(axis)
    pairs = [(i, i + by) for i in range(length) if 0 <= i + by < length]
    return lax.ppermute(x, axis, pairs)


def lower_solve(factor, right_side):
    return lax.linalg.triangular_solve(factor, right_side, left_side=True, lower=True)


def complex_product(matrix, vectors):
    block_order = matrix.shape[1]
    half_width = vectors.shape[1] // 2
    stacked = matrix.reshape(2 * block_order, block_order)
    stacked_out = jnp.dot(stacked, vectors.astype(jnp.bfloat16), preferred_element_type=jnp.float32)
    real_part = stacked_out[:block_order, :half_width] - stacked_out[block_order:, half_width:]
    imag_part = stacked_out[:block_order, half_width:] + stacked_out[block_order:, :half_width]
    return jnp.concatenate([real_part, imag_part], axis=1)


def real_product(matrix, vectors):
    return jnp.dot(matrix, vectors.astype(jnp.bfloat16), preferred_element_type=jnp.float32)


def transposed_product(matrix, vectors):
    return lax.dot_general(
        matrix,
        vectors.astype(jnp.bfloat16),
        (((0,), (0,)), ((), ())),
        preferred_element_type=jnp.float32,
    )


def inner_products(left, right_side):
    return lax.dot_general(
        left,
        right_side,
        (((0,), (0,)), ((), ())),
        precision=lax.Precision.HIGHEST,
        preferred_element_type=jnp.float32,
    )


def partition_solve(inverse, coupled, source):
    previous = jnp.roll(coupled, 1, axis=0)
    initial = jnp.zeros(source.shape[1:], jnp.float32)

    def forward_step(carried, members):
        block_inverse, given, couple_prev = members
        result = complex_product(block_inverse, given + transposed_product(couple_prev, carried))
        return (result, result)

    unused, forward = lax.scan(forward_step, initial, (inverse, source, previous))

    def backward_step(carried, members):
        block_inverse, partial_value, couple_next = members
        result = partial_value + complex_product(block_inverse, real_product(couple_next, carried))
        return (result, result)

    unused, backward = lax.scan(backward_step, initial, (inverse, forward, coupled), reverse=True)
    return backward


def on_device(initial_block, coupling, pivots, interface, pole_values):
    blocks = coupling.shape[1]
    coupled = coupling[0]
    inverse = pivots[0, 0]
    factors = interface[0, 0]
    real_start = initial_block[0].astype(jnp.float32)
    source = jnp.concatenate([real_start, jnp.zeros_like(real_start)], axis=-1)
    first = partition_solve(inverse, coupled, source)
    bottom = first[blocks - 1]
    top = first[0]
    top_next = shifted(top, "dom", -1)
    below = complex_product(factors[0], bottom) - complex_product(factors[1], top_next)
    topmost = lax.axis_index("dom") == lax.axis_size("dom") - 1
    above = jnp.where(
        topmost, jnp.zeros_like(top_next), top_next - complex_product(factors[2], below)
    )
    link = coupled[blocks - 1]
    lifted = transposed_product(link, below)
    arriving = shifted(lifted, "dom", 1)
    update = source.at[0].add(arriving)
    update = update.at[blocks - 1].add(real_product(link, above))
    second = partition_solve(inverse, coupled, update)
    real_z = pole_values[0, 0]
    imag_z = pole_values[0, 1]
    real_w = pole_values[0, 2]
    imag_w = pole_values[0, 3]
    real_x = second[..., :M]
    imag_x = second[..., M:]
    filtered_term = real_w * real_x - imag_w * imag_x
    shifted_term = (
        (real_w * real_z - imag_w * imag_z) * real_x
        - (real_w * imag_z + imag_w * real_z) * imag_x
        - real_w * real_start
    )
    count = blocks // lax.axis_size("pole")
    summed = lax.psum(filtered_term, "pole")
    offset = lax.axis_index("pole") * count
    own_rows = lax.dynamic_slice_in_dim(summed, offset, count, 0).reshape(count * B, M)
    gram_part = inner_products(own_rows, own_rows)
    projected_part = inner_products(
        summed.reshape(blocks * B, M), shifted_term.reshape(blocks * B, M)
    )
    gram_total, projected_total = lax.psum((gram_part, projected_part), ("pole", "dom"))
    row_total = blocks * B * lax.axis_size("dom")
    gram = gram_total / row_total
    projected = projected_total / row_total
    factor = jnp.linalg.cholesky(gram)
    filtered_basis = lower_solve(factor, own_rows.T).T.reshape(1, count, B, M)
    middle = lower_solve(factor, projected)
    rayleigh = lower_solve(factor, middle.T).T
    return (filtered_basis, rayleigh)


def solution(mesh):
    in_specs = (
        P("dom", None, None, None),
        P("dom", None, None, None),
        P("pole", "dom", None, None, None, None),
        P("pole", "dom", None, None, None, None),
        P("pole", None),
    )
    out_specs = (P("dom", "pole", None, None), P())
    return jax.shard_map(
        on_device, mesh=mesh, in_specs=in_specs, out_specs=out_specs, check_vma=False
    )
```

profile of v0, /device:TPU:0, one launch (start us, length us, event | category | flops | bytes accessed | tf_op | source)
XLA Modules:
  0.0 687.2 jit_solution(11109018124211285651)
XLA Ops:
  7.2 4.2 slice_bitcast_fusion
  12.5 2.9 copy.17
  18.0 4.2 concatenate.76
  22.3 2.3 pad_maximum_fusion.2
  24.6 4.3 broadcast.158.clone.2
  29.7 65.2 %while.65 = (s32[]{:T(128)}, bf16[512,512]{0,1:T(8,128)(2,1)}, f32[8,512,512]{1,2,0:T(8,128)}, bf16[8,2,512,512]{3,2,1,0:T(8,128)(2,1)}, f32[8,512,512]{1,2,0:T(8,128)}, /*index=5*/bf16[8,512,512]{2,1,0:T(8,128)(2,1)}, s32[]{:T(128)}) while((s32[]{:T(128)}, bf16[512,512]{0,1:T(8,128)(2,1)}, f32[8,512,512]{1,2,0:T(8,128)}, ...), condition=%wide.region_1.2_spmd, body=%wide.region_0.1_spmd.sunk | while | flops 806617088 | bytes 17302612 | solution.py:62
  33.6 2.7 fusion.145
  41.8 2.7 fusion.145
  50.0 2.7 fusion.145
  58.1 2.7 fusion.145
  66.3 2.7 fusion.145
  74.5 2.7 fusion.145
  82.6 2.7 fusion.145
  90.7 2.7 fusion.145
  95.0 4.3 broadcast.158.clone.1
  99.3 67.7 %while.68 = (s32[]{:T(128)}, bf16[512,512]{0,1:T(8,128)(2,1)}, f32[8,512,512]{1,2,0:T(8,128)}, f32[8,512,512]{1,2,0:T(8,128)}, bf16[8,2,512,512]{3,2,1,0:T(8,128...) while((s32[]{:T(128)}, bf16[512,512]{0,1:T(8,128)(2,1)}, ...), condition=%wide.region_3.4_spmd.clone, body=%wide.region_2.3_spmd.clone.sunk | while | flops 807403520 | bytes 15204483 | solution.py:69
  103.0 2.5 fusion.154
  109.0 2.3 fusion.153
  111.5 2.4 fusion.154
  120.0 2.4 fusion.154
  128.5 2.4 fusion.154
  136.9 2.4 fusion.154
  142.9 2.3 fusion.153
  145.4 2.4 fusion.154
  153.9 2.4 fusion.154
  162.4 2.4 fusion.154
  173.8 22.5 %collective-permute-done = f32[512,512]{0,1:T(8,128)S(1)} collective-permute-done((f32[512,512]{0,1:T(8,128)S(1)}, f32[512,512]{0,1:T(8,128)S(1)}, u32[]{:S(2)}, u32[]{:S(2)}) %collective-permute-start) | collective-permute-done | bytes 1048608 | tf_op jit(solution)/shard_map/ppermute | solution.py:13
  197.6 2.5 convolution_bitcast_fusion.4
  200.0 6.1 collective-permute-start.1
  207.7 18.7 %collective-permute-done.1 = f32[512,512]{0,1:T(8,128)} collective-permute-done((f32[512,512]{0,1:T(8,128)}, f32[512,512]{0,1:T(8,128)}, u32[]{:S(2)}, u32[]{:S(2)}) %collective-permute-start.1) | collective-permute-done | bytes 1048608 | tf_op jit(solution)/shard_map/ppermute | solution.py:13
  226.4 2.3 fusion.65
  228.8 2.9 fusion.66
  231.7 4.3 broadcast.158.clone
  236.8 65.4 %while.66 = (s32[]{:T(128)}, bf16[512,512]{0,1:T(8,128)(2,1)}, f32[8,512,512]{1,2,0:T(8,128)}, bf16[8,2,512,512]{3,2,1,0:T(8,128)(2,1)}, f32[8,512,512]{1,2,0:T(8,128)}, /*index=5*/bf16[8,512,512]{2,1,0:T(8,128)(2,1)}, s32[]{:T(128)}) while((s32[]{:T(128)}, bf16[512,512]{0,1:T(8,128)(2,1)}, f32[8,512,512]{1,2,0:T(8,128)}, ...), condition=%wide.region_5.6_spmd, body=%wide.region_4.5_spmd.sunk | while | flops 806617088 | bytes 17302612 | solution.py:62
  240.7 2.7 fusion.149
  248.9 2.7 fusion.149
  257.0 2.7 fusion.149
  265.2 2.7 fusion.149
  273.4 2.7 fusion.149
  281.7 2.7 fusion.149
  289.9 2.7 fusion.149
  298.0 2.7 fusion.149
  302.3 4.3 broadcast.158
  306.6 67.7 %while.69 = (s32[]{:T(128)}, bf16[512,512]{0,1:T(8,128)(2,1)}, f32[8,512,512]{1,2,0:T(8,128)}, f32[8,512,512]{1,2,0:T(8,128)}, bf16[8,2,512,512]{3,2,1,0:T(8,128...) while((s32[]{:T(128)}, bf16[512,512]{0,1:T(8,128)(2,1)}, ...), condition=%wide.region_7.8_spmd.clone, body=%wide.region_6.7_spmd.clone.sunk | while | flops 807403520 | bytes 15204483 | solution.py:69
  310.3 2.5 fusion.158
  316.3 2.3 fusion.157
  318.8 2.4 fusion.158
  324.7 2.3 fusion.157
  327.3 2.4 fusion.158
  335.8 2.4 fusion.158
  344.2 2.4 fusion.158
  350.2 2.3 fusion.157
  352.7 2.4 fusion.158
  361.2 2.4 fusion.158
  369.6 2.4 fusion.158
  374.3 7.7 %multiply_subtract_fusion = f32[8,512,256]{1,2,0:T(8,128)} fusion(f32[8,512,512]{1,2,0:T(8,128)} %get-tuple-element.338, f32[]{:T(128)} %bitcast.27, f32[]{:T(128)} %bitcast.8), kind=kLoop, calls=%fused_computation.67 | loop fusion | flops 3145728 | bytes 12582920 | tf_op jit(solution)/shard_map/sub | solution.py:101
  387.1 81.9 %all-reduce.6.cloned.1.call-done = f32[8,512,256]{1,2,0:T(8,128)} async-done(((f32[8,512,256]{1,2,0:T(8,128)}), f32[8,512,256]{1,2,0:T(8,128)}) %all-reduce.6.cloned.1.call-update) | async-done | bytes 4194320 | tf_op jit(solution)/shard_map/psum | solution.py:108
  472.1 9.1 %fusion.61 = f32[256,256]{0,1:T(8,128)} fusion(f32[8,512,256]{1,2,0:T(8,128)S(1)} %copy-done.5, f32[8,512,512]{1,2,0:T(8,128)} %get-tuple-element.338, f32[]{:T(128)S(6)} %add.171, f32[]{:T(128)S(6)} %sub.71, f32[]{:T(128)} %bitcast.8, bf16[1,8,512,256]{2,3,1,0:T(8,128)(2,1)S(1)} %copy-done.3), kind=kOutput, calls=%fused_computation.82 | convolution fusion | flops 3227516928 | bytes 14942220 | tf_op jit(solution)/shard_map/dot_general | solution.py:44
  481.6 129.2 %all-reduce.8.cloned.1.call-done = (f32[256,256]{0,1:T(8,128)}, f32[256,256]{0,1:T(8,128)}) async-done(((f32[256,256]{0,1:T(8,128)}, f32[256,256]{0,1:T(8,128)}), (f32[256,256]{0,1:T(8,128)}, f32[256,256]{0,1:T(8,128)})) %all-reduce.8.cloned.1.call-update) | async-done | bytes 524304 | tf_op jit(solution)/shard_map/psum | solution.py:115
  613.1 11.7 %cholesky.50 = f32[128,128]{1,0:T(8,128)S(1)} custom-call(f32[128,128]{1,0:T(8,128)S(1)} %cholesky.118), custom_call_target="Cholesky" | custom-call | tf_op jit(solution)/shard_map/jit(cholesky)/cholesky | solution.py:119
  624.8 10.0 %custom-call.17 = f32[1,128,128]{1,2,0:T(8,128)S(1)} custom-call(f32[1,128,128]{2,1,0:T(8,128)S(1)} %get-tuple-element.517), custom_call_target="InvertDiagBlocksLowerTriangular" | custom-call | tf_op jit(solution)/shard_map/jit(cholesky)/cholesky | solution.py:119
  635.3 11.7 %cholesky.105 = f32[128,128]{1,0:T(8,128)S(1)} custom-call(f32[128,128]{1,0:T(8,128)S(1)} %convolution_subtract_fusion.3), custom_call_target="Cholesky" | custom-call | tf_op jit(solution)/shard_map/jit(cholesky)/cholesky | solution.py:119
  649.8 4.0 while.67
  653.7 19.7 %custom-call.18 = f32[2,128,128]{1,2,0:T(8,128)S(1)} custom-call(f32[2,128,128]{2,1,0:T(8,128)S(1)} %get-tuple-element.354), custom_call_target="InvertDiagBlocksLowerTriangular" | custom-call | tf_op jit(solution)/shard_map/triangular_solve | solution.py:17
  (212 shorter events, 205.6 us)
Async XLA Ops:
  7.2 461.8 %all-reduce.6.cloned.1.call-start = ((), (), s32[]{:S(2)}) async-start(), calls=%async_computation | async-start | bytes 8388608 | tf_op jit(solution)/shard_map/psum | solution.py:108
  15.4 6.9 %copy-start.2 = (bf16[1,8,512,256]{2,3,1,0:T(8,128)(2,1)}, bf16[1,8,512,256]{2,3,1,0:T(8,128)(2,1)S(1)}, u32[]{:S(2)}) copy-start(bf16[1,8,512,256]{2,3,1,0:T(8,128)(2,1)S(1)} %copy.17) | copy-start | bytes 6291460
  15.9 2.1 copy-start
  18.0 4.2 copy-start.4
  168.3 28.0 %collective-permute-start = (f32[512,512]{0,1:T(8,128)S(1)}, f32[512,512]{0,1:T(8,128)S(1)}, u32[]{:S(2)}, u32[]{:S(2)}) collective-permute-start(f32[512,512]{0,1:T(8,128)S(1)} %slice_bitcast_fusion.1), channel_id=1, source_target_pairs={{1,0},{2,1},{3,2},{4,3},{5,4},{6,5},{7,6},{9,8},{10,9},{11,10},{12... | collective-permute-start | bytes 3145736 | tf_op jit(solution)/shard_map/ppermute | solution.py:13
  197.1 9.1 %copy-start.6 = (f32[1,4]{1,0:T(1,128)S(1)}, f32[1,4]{1,0:T(1,128)}, u32[]{:S(2)}) copy-start(f32[1,4]{1,0:T(1,128)} %param.23) | copy-start | bytes 52
  200.0 26.4 %collective-permute-start.1 = (f32[512,512]{0,1:T(8,128)}, f32[512,512]{0,1:T(8,128)}, u32[]{:S(2)}, u32[]{:S(2)}) collective-permute-start(f32[512,512]{0,1:T(8,128)} %convolution_bitcast_fusion.4), channel_id=1, source_target_pairs={{0,1},{1,2},{2,3},{3,4},{4,5},{5,6},{6,7},{8,9},{9,10},{10,11},{11... | collective-permute-start | bytes 3145736 | tf_op jit(solution)/shard_map/ppermute | solution.py:13
  206.1 20.3 %copy-start.1 = (f32[8,512,256]{1,2,0:T(8,128)S(1)}, f32[8,512,256]{1,2,0:T(8,128)}, u32[]{:S(2)}) copy-start(f32[8,512,256]{1,2,0:T(8,128)} %copy-done) | copy-start | bytes 12582916
  382.0 90.2 %copy-start.3 = (bf16[1,8,512,256]{2,3,1,0:T(8,128)(2,1)S(1)}, bf16[1,8,512,256]{2,3,1,0:T(8,128)(2,1)}, u32[]{:S(2)}) copy-start(bf16[1,8,512,256]{2,3,1,0:T(8,128)(2,1)} %copy-done.2) | copy-start | bytes 6291460
  382.0 228.9 %all-reduce.8.cloned.1.call-start = ((), (), s32[]{:S(2)}) async-start(), calls=%async_computation.1 | async-start | bytes 1048576 | tf_op jit(solution)/shard_map/psum | solution.py:115
  469.0 3.2 copy-start.5
Sparse Core Ops, SparseCore 0:
  382.1 86.7 all-reduce.5
  481.4 129.4 all-reduce.7
where the time goes:
time: 699 us; the launch traced here: 687 us
  waiting for transfers between devices  252 us (36%)
  other arithmetic  173 us (25%)
  local copies, waits for them, and re-layouts  128 us (18%)
  matrix products  104 us (15%)
  between operations  20.8 us (3%)
  starting transfers between devices  7.59 us (1%)
    psum x1, waiting for transfers between devices, on_device(): lax.psum((gram_part, projected_part), ('pole', 'dom'))  129 us
    dot_general x35, matrix products, complex_product(): jnp.dot(stacked, vectors.astype(jnp.bfloat16), preferred_element_type=jnp...  83.1 us
    dynamic_slice x64, local copies, waits for them, and re-layouts, partition_solve(): lax.scan(forward_step, initial, (inverse, source, previous))  82.9 us
    psum x1, waiting for transfers between devices, on_device(): summed = lax.psum(filtered_term, 'pole')  81.9 us
    dynamic_update_slice x32, other arithmetic, partition_solve(): lax.scan(forward_step, initial, (inverse, source, previous))  60.9 us
    ppermute x2, waiting for transfers between devices, shifted(): return lax.ppermute(x, axis, pairs)  41.1 us
    add x16, other arithmetic, backward_step(): partial_value + complex_product(block_inverse, real_product(couple_next,...  35.2 us
    another operation x7, other arithmetic, on_device(): factor = jnp.linalg.cholesky(gram)  34.8 us
  transfers between devices with their start and end apart: 4, of which 4 were waited for; matrix products, arithmetic and copies ran while one was open for 1% of the time, Pallas kernels for 0%

commit v1 on v0

--- a/solution.py
+++ b/solution.py
@@ -105,7 +105,8 @@
         - real_w * real_start
     )
     count = blocks // lax.axis_size("pole")
-    summed = lax.psum(filtered_term, "pole")
+    terms = lax.all_gather(filtered_term, "pole")
+    summed = jnp.sum(terms, axis=0)
     offset = lax.axis_index("pole") * count
     own_rows = lax.dynamic_slice_in_dim(summed, offset, count, 0).reshape(count * B, M)
     gram_part = inner_products(own_rows, own_rows)

time: 699 us -> 735 us (1.052)
  waiting for transfers between devices: 252 us -> 273 us
  other arithmetic: 173 us -> 183 us
    all_gather x0 -> x1, waiting for transfers between devices: none -> 102 us  [on_device(): terms = lax.all_gather(filtered_term, 'pole')]
    psum x1 -> x0, waiting for transfers between devices: 81.9 us -> none  [on_device(): summed = lax.psum(filtered_term, 'pole')]
    unnamed x3 -> x4, other arithmetic: 0.01 us -> 9.72 us
where the time goes in v1:
time: 735 us; the launch traced here: 724 us
  waiting for transfers between devices  273 us (37%)
  other arithmetic  183 us (25%)
  local copies, waits for them, and re-layouts  133 us (18%)
  matrix products  105 us (14%)
  between operations  20.7 us (3%)
  starting transfers between devices  7.77 us (1%)
    psum x1, waiting for transfers between devices, on_device(): lax.psum((gram_part, projected_part), ('pole', 'dom'))  129 us
    all_gather x1, waiting for transfers between devices, on_device(): terms = lax.all_gather(filtered_term, 'pole')  102 us
    dot_general x35, matrix products, complex_product(): jnp.dot(stacked, vectors.astype(jnp.bfloat16), preferred_element_type=jnp...  83.1 us
    dynamic_slice x64, local copies, waits for them, and re-layouts, partition_solve(): lax.scan(forward_step, initial, (inverse, source, previous))  82.9 us
    dynamic_update_slice x32, other arithmetic, partition_solve(): lax.scan(forward_step, initial, (inverse, source, previous))  60.9 us
    ppermute x2, waiting for transfers between devices, shifted(): return lax.ppermute(x, axis, pairs)  41.3 us
    add x16, other arithmetic, backward_step(): partial_value + complex_product(block_inverse, real_product(couple_next,...  35.3 us
    another operation x7, other arithmetic, on_device(): factor = jnp.linalg.cholesky(gram)  34.7 us
  transfers between devices with their start and end apart: 4, of which 4 were waited for; matrix products, arithmetic and copies ran while one was open for 1% of the time, Pallas kernels for 0%

profile of v1, /device:TPU:0, one launch (start us, length us, event | category | flops | bytes accessed | tf_op | source)
XLA Modules:
  0.0 723.7 jit_solution(5081764581090901401)
XLA Ops:
  7.2 4.2 slice_bitcast_fusion
  12.5 2.9 copy.18
  18.0 4.2 concatenate.76
  22.3 2.3 pad_maximum_fusion.2
  24.6 4.3 broadcast.158.clone.2
  29.7 65.2 %while.65 = (s32[]{:T(128)}, bf16[512,512]{0,1:T(8,128)(2,1)}, f32[8,512,512]{1,2,0:T(8,128)}, bf16[8,2,512,512]{3,2,1,0:T(8,128)(2,1)}, f32[8,512,512]{1,2,0:T(8,128)}, /*index=5*/bf16[8,512,512]{2,1,0:T(8,128)(2,1)}, s32[]{:T(128)}) while((s32[]{:T(128)}, bf16[512,512]{0,1:T(8,128)(2,1)}, f32[8,512,512]{1,2,0:T(8,128)}, ...), condition=%wide.region_1.2_spmd, body=%wide.region_0.1_spmd.sunk | while | flops 806617088 | bytes 17302612 | solution.py:62
  33.6 2.7 fusion.145
  41.8 2.7 fusion.145
  50.0 2.7 fusion.145
  58.1 2.7 fusion.145
  66.3 2.7 fusion.145
  74.5 2.7 fusion.145
  82.6 2.7 fusion.145
  90.7 2.7 fusion.145
  95.0 4.3 broadcast.158.clone.1
  99.3 67.7 %while.68 = (s32[]{:T(128)}, bf16[512,512]{0,1:T(8,128)(2,1)}, f32[8,512,512]{1,2,0:T(8,128)}, f32[8,512,512]{1,2,0:T(8,128)}, bf16[8,2,512,512]{3,2,1,0:T(8,128...) while((s32[]{:T(128)}, bf16[512,512]{0,1:T(8,128)(2,1)}, ...), condition=%wide.region_3.4_spmd.clone, body=%wide.region_2.3_spmd.clone.sunk | while | flops 807403520 | bytes 15204483 | solution.py:69
  103.0 2.5 fusion.154
  111.5 2.4 fusion.154
  120.0 2.4 fusion.154
  128.5 2.4 fusion.154
  136.9 2.4 fusion.154
  145.4 2.4 fusion.154
  153.9 2.4 fusion.154
  162.4 2.4 fusion.154
  173.8 22.5 %collective-permute-done = f32[512,512]{0,1:T(8,128)S(1)} collective-permute-done((f32[512,512]{0,1:T(8,128)S(1)}, f32[512,512]{0,1:T(8,128)S(1)}, u32[]{:S(2)}, u32[]{:S(2)}) %collective-permute-start) | collective-permute-done | bytes 1048608 | tf_op jit(solution)/shard_map/ppermute | solution.py:13
  197.6 2.5 convolution_bitcast_fusion.4
  200.0 5.9 collective-permute-start.1
  207.6 18.9 %collective-permute-done.1 = f32[512,512]{0,1:T(8,128)} collective-permute-done((f32[512,512]{0,1:T(8,128)}, f32[512,512]{0,1:T(8,128)}, u32[]{:S(2)}, u32[]{:S(2)}) %collective-permute-start.1) | collective-permute-done | bytes 1048608 | tf_op jit(solution)/shard_map/ppermute | solution.py:13
  226.4 2.3 fusion.65
  228.8 2.9 fusion.66
  231.7 4.3 broadcast.158.clone
  236.8 65.4 %while.66 = (s32[]{:T(128)}, bf16[512,512]{0,1:T(8,128)(2,1)}, f32[8,512,512]{1,2,0:T(8,128)}, bf16[8,2,512,512]{3,2,1,0:T(8,128)(2,1)}, f32[8,512,512]{1,2,0:T(8,128)}, /*index=5*/bf16[8,512,512]{2,1,0:T(8,128)(2,1)}, s32[]{:T(128)}) while((s32[]{:T(128)}, bf16[512,512]{0,1:T(8,128)(2,1)}, f32[8,512,512]{1,2,0:T(8,128)}, ...), condition=%wide.region_5.6_spmd, body=%wide.region_4.5_spmd.sunk | while | flops 806617088 | bytes 17302612 | solution.py:62
  240.7 2.7 fusion.149
  248.9 2.7 fusion.149
  257.0 2.7 fusion.149
  265.2 2.7 fusion.149
  273.4 2.7 fusion.149
  281.7 2.7 fusion.149
  289.9 2.7 fusion.149
  298.0 2.7 fusion.149
  302.3 4.3 broadcast.158
  306.6 67.8 %while.69 = (s32[]{:T(128)}, bf16[512,512]{0,1:T(8,128)(2,1)}, f32[8,512,512]{1,2,0:T(8,128)}, f32[8,512,512]{1,2,0:T(8,128)}, bf16[8,2,512,512]{3,2,1,0:T(8,128...) while((s32[]{:T(128)}, bf16[512,512]{0,1:T(8,128)(2,1)}, ...), condition=%wide.region_7.8_spmd.clone, body=%wide.region_6.7_spmd.clone.sunk | while | flops 807403520 | bytes 15204483 | solution.py:69
  310.3 2.5 fusion.158
  316.3 2.3 fusion.157
  318.8 2.4 fusion.158
  327.3 2.4 fusion.158
  333.3 2.3 fusion.157
  335.8 2.4 fusion.158
  344.3 2.4 fusion.158
  352.8 2.4 fusion.158
  361.3 2.4 fusion.158
  369.7 2.4 fusion.158
  374.4 7.6 %multiply_subtract_fusion = f32[8,512,256]{1,2,0:T(8,128)} fusion(f32[8,512,512]{1,2,0:T(8,128)} %get-tuple-element.338, f32[]{:T(128)} %bitcast.27, f32[]{:T(128)} %bitcast.8), kind=kLoop, calls=%fused_computation.67 | loop fusion | flops 3145728 | bytes 12582920 | tf_op jit(solution)/shard_map/sub | solution.py:101
  382.0 5.4 copy.21
  392.8 102.0 %all-gather.3.cloned.1.call-done = f32[32,512,256]{2,1,0:T(8,128)} async-done(((f32[8,512,256]{2,1,0:T(8,128)}), f32[32,512,256]{2,1,0:T(8,128)}) %all-gather.3.cloned.1.call-update) | async-done | bytes 16777232 | tf_op jit(solution)/shard_map/all_gather | solution.py:108
  494.8 9.7 %reduce_sum.9 = f32[8,512,256]{2,1,0:T(8,128)} reduce(f32[4,8,512,256]{3,2,1,0:T(8,128)} %bitcast.224, f32[]{:T(128)} %constant.243.clone.1), dimensions={0}, to_apply=%region_8.9 | reduce | flops 3145728 | bytes 20971524
  506.0 2.5 convolution_bitcast_fusion.5
  508.5 9.3 %fusion.61 = f32[256,256]{0,1:T(8,128)} fusion(f32[8,512,256]{2,1,0:T(8,128)S(1)} %copy-done.2, f32[8,512,512]{1,2,0:T(8,128)} %get-tuple-element.338, f32[]{:T(128)S(6)} %add.169, f32[]{:T(128)S(6)} %sub.71, f32[]{:T(128)} %bitcast.8, bf16[1,8,512,256]{2,3,1,0:T(8,128)(2,1)S(1)} %copy-done.4), kind=kOutput, calls=%fused_computation.82 | convolution fusion | flops 3227516928 | bytes 14942220 | tf_op jit(solution)/shard_map/dot_general | solution.py:44
  517.8 129.5 %all-reduce.5.cloned.1.call-done = (f32[256,256]{0,1:T(8,128)}, f32[256,256]{0,1:T(8,128)}) async-done(((f32[256,256]{0,1:T(8,128)}, f32[256,256]{0,1:T(8,128)}), (f32[256,256]{0,1:T(8,128)}, f32[256,256]{0,1:T(8,128)})) %all-reduce.5.cloned.1.call-update) | async-done | bytes 524304 | tf_op jit(solution)/shard_map/psum | solution.py:116
  649.4 11.9 %cholesky.50 = f32[128,128]{1,0:T(8,128)S(1)} custom-call(f32[128,128]{1,0:T(8,128)S(1)} %cholesky.118), custom_call_target="Cholesky" | custom-call | tf_op jit(solution)/shard_map/jit(cholesky)/cholesky | solution.py:120
  661.4 9.8 %custom-call.17 = f32[1,128,128]{1,2,0:T(8,128)S(1)} custom-call(f32[1,128,128]{2,1,0:T(8,128)S(1)} %get-tuple-element.517), custom_call_target="InvertDiagBlocksLowerTriangular" | custom-call | tf_op jit(solution)/shard_map/jit(cholesky)/cholesky | solution.py:120
  671.7 11.7 %cholesky.105 = f32[128,128]{1,0:T(8,128)S(1)} custom-call(f32[128,128]{1,0:T(8,128)S(1)} %convolution_subtract_fusion.3), custom_call_target="Cholesky" | custom-call | tf_op jit(solution)/shard_map/jit(cholesky)/cholesky | solution.py:120
  686.1 4.2 while.67
  690.3 19.7 %custom-call.18 = f32[2,128,128]{1,2,0:T(8,128)S(1)} custom-call(f32[2,128,128]{2,1,0:T(8,128)S(1)} %get-tuple-element.354), custom_call_target="InvertDiagBlocksLowerTriangular" | custom-call | tf_op jit(solution)/shard_map/triangular_solve | solution.py:17
  (213 shorter events, 210.9 us)
Async XLA Ops:
  7.2 487.6 %all-gather.3.cloned.1.call-start = ((), (), s32[]{:S(2)}) async-start(), calls=%async_computation | async-start | bytes 20971520 | tf_op jit(solution)/shard_map/all_gather | solution.py:108
  15.4 6.9 copy-start.3
  15.9 2.1 copy-start
  18.0 4.2 copy-start.5
  168.3 28.0 %collective-permute-start = (f32[512,512]{0,1:T(8,128)S(1)}, f32[512,512]{0,1:T(8,128)S(1)}, u32[]{:S(2)}, u32[]{:S(2)}) collective-permute-start(f32[512,512]{0,1:T(8,128)S(1)} %slice_bitcast_fusion.1), channel_id=1, source_target_pairs={{1,0},{2,1},{3,2},{4,3},{5,4},{6,5},{7,6},{9,8},{10,9},{11,10},{12... | collective-permute-start | bytes 3145736 | tf_op jit(solution)/shard_map/ppermute | solution.py:13
  197.1 8.9 %copy-start.6 = (f32[1,4]{1,0:T(1,128)S(1)}, f32[1,4]{1,0:T(1,128)}, u32[]{:S(2)}) copy-start(f32[1,4]{1,0:T(1,128)} %param.23) | copy-start | bytes 52
  200.0 26.4 %collective-permute-start.1 = (f32[512,512]{0,1:T(8,128)}, f32[512,512]{0,1:T(8,128)}, u32[]{:S(2)}, u32[]{:S(2)}) collective-permute-start(f32[512,512]{0,1:T(8,128)} %convolution_bitcast_fusion.4), channel_id=1, source_target_pairs={{0,1},{1,2},{2,3},{3,4},{4,5},{5,6},{6,7},{8,9},{9,10},{10,11},{11... | collective-permute-start | bytes 3145736 | tf_op jit(solution)/shard_map/ppermute | solution.py:13
  206.0 20.5 %copy-start.1 = (f32[8,512,256]{1,2,0:T(8,128)S(1)}, f32[8,512,256]{1,2,0:T(8,128)}, u32[]{:S(2)}) copy-start(f32[8,512,256]{1,2,0:T(8,128)} %copy-done) | copy-start | bytes 12582916
  387.4 259.8 %all-reduce.5.cloned.1.call-start = ((), (), s32[]{:S(2)}) async-start(), calls=%async_computation.1 | async-start | bytes 1048576 | tf_op jit(solution)/shard_map/psum | solution.py:116
  494.8 13.7 %copy-start.4 = (bf16[1,8,512,256]{2,3,1,0:T(8,128)(2,1)S(1)}, bf16[1,8,512,256]{2,3,1,0:T(8,128)(2,1)}, u32[]{:S(2)}) copy-start(bf16[1,8,512,256]{2,3,1,0:T(8,128)(2,1)} %copy-done.3) | copy-start | bytes 6291460
  504.5 4.0 copy-start.2
Sparse Core Ops, SparseCore 0:
  387.5 107.2 all-gather.2
  517.9 129.3 all-reduce.4
